TPU v7x, 32 devices: a whole 2x2x4 slice. The times are simulated.
32 devices in a mesh: gx: 4 (over z), gy: 4 (over y, core), gz: 2 (over x).
Axes of the slice: x: 2, y: 2, z: 4, core: 2. Of those that a mesh axis runs over, the one named last changes fastest.
Arguments:
- positions_now: float32 [32, 16, 2, 4, 128], P('gx', 'gy', 'gz'), may hold values from 0 to 1
- velocities: float32 [32, 16, 2, 3, 128], P('gx', 'gy', 'gz'), may hold values from -6 to 6
- positions_next: float32 [32, 16, 2, 3, 128], P('gx', 'gy', 'gz'), may hold values from 0 to 1
- halo_counts: int32 [32, 16, 2], P('gx', 'gy', 'gz'), may hold values from 1 to 128, as said below
- neighbour_lists: int32 [32, 16, 2, 14], P('gx', 'gy', 'gz'), may hold values from 0 to 26, as said below
- descendants: int32 [32, 16, 2, 2, 128], P('gx', 'gy', 'gz'), may hold values from 0 to 127, as said below
Outputs:
- drift: float32 [32, 16, 2, 3, 128], P('gx', 'gy', 'gz')
- tension: float32 [32, 16, 2, 128], P('gx', 'gy', 'gz')
Inputs may be any that keep to these rules, and one draw needn't show every extreme that they name: `halo_counts`: every cell holds 1 to 128 live halos; some cell holds exactly 128. `neighbour_lists`: each cell's list begins with code 13 (the cell itself) and holds distinct codes. `descendants`: row 0 is a code 0 to 26; row 1 is a live slot of the descendant's cell.
All inputs are finite; a program needn't handle non-finite values.
Results may differ from a plain program's by a relative error of at most 0.0003.
Values sent between devices are 32-bit elements; how exact they have to be, the bound alone decides.
A program may use at most 64 MiB of HBM per device.

v0:
```python
import functools

import jax
import jax.numpy as jnp
from jax import lax
from jax.experimental import pallas as pl
from jax.experimental.pallas import tpu as pltpu
from jax.sharding import PartitionSpec as P

EPS_SQ = 0.01
STEP_DT = 0.3
HALF_KICK = 0.045
SPAN = 4


def shifted(shard, axis, by):
    peers = lax.axis_size(axis)
    return lax.ppermute(shard, axis, [(i, (i + by) % peers) for i in range(peers)])


def pieces(tile):
    first = tile.astype(jnp.bfloat16).astype(jnp.float32)
    rest = tile - first
    second = rest.astype(jnp.bfloat16).astype(jnp.float32)
    return first, second, rest - second


def kernel(dims, width, lists, padded, vel, desc, drift_ref, sq_ref, stat_ref, placed, packed, counts):
    cx, cy, cz = dims
    py, pz = cy + 2, cz + 2
    cells = cx * cy * cz
    slots = padded.shape[-1]
    row = lax.broadcasted_iota(jnp.int32, (8, slots), 0)
    lane = lax.broadcasted_iota(jnp.int32, (8, slots), 1)
    wide = SPAN * slots
    wrow = lax.broadcasted_iota(jnp.int32, (8, wide), 0)

    def place(n, _):
        ix, iy, iz = n // (py * pz), n // pz % py, n % pz
        fx = ix.astype(jnp.float32) - (cx + 2) / 2
        fy = iy.astype(jnp.float32) - (cy + 2) / 2
        fz = iz.astype(jnp.float32) - (cz + 2) / 2
        shift = jnp.where(row % 4 == 0, fx, jnp.where(row % 4 == 1, fy, jnp.where(row % 4 == 2, fz, 0.0)))
        tile = padded[n]
        placed[n] = tile + shift
        counts[n] = jnp.max(tile[7:8]).astype(jnp.int32)
        return 0

    lax.fori_loop(0, padded.shape[0], place, 0, unroll=6)

    def target(n, stats):
        ix, iy, iz = n // (cy * cz), n // cz % cy, n % cz
        corner = (ix * py + iy) * pz + iz
        base = corner + (py + 1) * pz + 1
        own = placed[base]
        count = counts[base]

        def source(k):
            code = lists[n * width + k]
            d9 = (code * 57) >> 9
            d3 = (code * 43) >> 7
            return corner + d9 * (py * pz) + (d3 - 3 * d9) * pz + code - 3 * d3

        at = jnp.int32(0)
        for k in range(width):
            cell = source(k)
            q, by = at // slots, at % slots
            turned = pltpu.roll(placed[cell], by, 1)
            packed[q] = jnp.where(lane >= by, turned, packed[q])
            packed[q + 1] = turned
            at = at + counts[cell]
        q, by = at // slots, at % slots
        packed[q] = jnp.where(lane >= by, 0.0, packed[q])
        for k in range(1, SPAN):
            packed[q + k] = jnp.zeros_like(own)
        chunks = (at + wide - 1) // wide

        norm = own[0:1] * own[0:1] + own[1:2] * own[1:2] + own[2:3] * own[2:3]
        ext = jnp.where(row < 3, -2.0 * own, jnp.where(row == 3, 1.0, jnp.where(row == 4, norm + EPS_SQ, 0.0)))
        a, b, c = pieces(ext)
        lhs = jnp.concatenate([a, b, c, a, b, a], axis=0).T.astype(jnp.bfloat16)

        def chunk(rows, m, acc):
            tile = jnp.concatenate([packed[m * SPAN + k] for k in range(SPAN)], axis=1)
            mass = tile[3:4]
            size = tile[0:1] * tile[0:1] + tile[1:2] * tile[1:2] + tile[2:3] * tile[2:3]
            x = jnp.where(wrow < 3, tile, jnp.where(wrow == 3, size, jnp.where(wrow == 4, 1.0, 0.0)))
            a, b, c = pieces(x)
            f = jnp.concatenate([a, a, a, b, b, c], axis=0).astype(jnp.bfloat16)
            mom = jnp.where(wrow < 3, tile * mass, jnp.where(wrow == 3, mass, 0.0))
            z = jnp.concatenate(list(pieces(mom)) + [jnp.zeros_like(mom)], axis=0).astype(jnp.bfloat16)
            dist_sq = jnp.dot(lhs[:rows], f, preferred_element_type=jnp.float32)
            inv = lax.rsqrt(dist_sq)
            weight = inv * inv * inv
            high = weight.astype(jnp.bfloat16)
            low = (weight - high.astype(jnp.float32)).astype(jnp.bfloat16)
            dn = (((1,), (1,)), ((), ()))
            acc += lax.dot_general(high, z, dn, preferred_element_type=jnp.float32)
            acc += lax.dot_general(low, z, dn, preferred_element_type=jnp.float32)
            return acc

        def attract(rows):
            acc = lax.fori_loop(
                0, chunks, functools.partial(chunk, rows), jnp.zeros((rows, 32), jnp.float32)
            )
            if rows < slots:
                acc = jnp.concatenate([acc, jnp.zeros((slots - rows, 32), jnp.float32)], axis=0)
            return acc

        acc = lax.cond(count > slots // 2, lambda: attract(slots), lambda: attract(slots // 2))
        acc = acc.T
        sums = acc[0:8] + acc[8:16] + acc[16:24]
        accel = sums[0:3] - own[0:3] * sums[3:4]
        predicted = own[0:3] + STEP_DT * vel[n] + HALF_KICK * accel
        links = desc[n]
        dcode = jnp.broadcast_to(links[0:1], (8, slots))
        dslot = jnp.broadcast_to(links[1:2], (8, slots))
        found = jnp.zeros((8, slots), jnp.float32)
        for code in range(27):
            near = corner + (code // 9) * py * pz + (code // 3 % 3) * pz + code % 3
            got = jnp.take_along_axis(placed[near], dslot, axis=1)
            found = jnp.where(dcode == code, got, found)
        live = lane[0:1] < count
        error = jnp.where(live, found[4:7] - predicted, 0.0)
        drift_ref[n] = error
        squared = jnp.sum(error * error, axis=0, keepdims=True)
        sq_ref[pl.ds(n, 1), :] = squared
        return stats + jnp.where(row == 0, squared, jnp.where((row == 1) & live, 1.0, 0.0))

    stat_ref[...] = lax.fori_loop(0, cells, target, jnp.zeros((8, slots), jnp.float32))[0:2]


def scale_kernel(axes, sizes, stat, squared, out, inbox, send_sem, recv_sem):
    total = 1
    me = 0
    for name, size in zip(axes, sizes):
        total *= size
        me = me * size + lax.axis_index(name)

    def peer(step):
        at = lax.rem(me + step, total)
        where = []
        for size in reversed(sizes):
            where.append(lax.rem(at, size))
            at = at // size
        return tuple(reversed(where))

    barrier = pltpu.get_barrier_semaphore()

    def greet(step, _):
        pl.semaphore_signal(barrier, inc=1, device_id=peer(step), device_id_type=pl.DeviceIdType.MESH)
        return 0

    lax.fori_loop(1, total, greet, 0)
    pl.semaphore_wait(barrier, total - 1)

    def send(step, _):
        pltpu.make_async_remote_copy(
            src_ref=stat,
            dst_ref=inbox.at[step - 1],
            send_sem=send_sem,
            recv_sem=recv_sem,
            device_id=peer(step),
            device_id_type=pl.DeviceIdType.MESH,
        ).start()
        return 0

    lax.fori_loop(1, total, send, 0)
    pltpu.make_async_copy(inbox, inbox, recv_sem).wait()
    sums = stat[...] + jnp.sum(inbox[...], axis=0)
    mean_sq = jnp.sum(sums[0:1], axis=1, keepdims=True) / jnp.sum(sums[1:2], axis=1, keepdims=True)
    out[...] = squared[...] / (mean_sq + 1e-06)
    pltpu.make_async_copy(inbox, inbox, send_sem).wait()


def shards(positions_now, velocities, positions_next, halo_counts, neighbour_lists, descendants):
    slots = positions_now.shape[-1]
    cx, cy, cz, width = neighbour_lists.shape
    cells = cx * cy * cz
    live = (
        jnp.arange(slots, dtype=jnp.int32)[None, None, None, :] < halo_counts[..., None]
    ).astype(jnp.float32)
    lv = live[:, :, :, None, :]
    tally = halo_counts[:, :, :, None, None].astype(jnp.float32)
    state = jnp.concatenate(
        [positions_now[:, :, :, :3, :], positions_now[:, :, :, 3:4, :] * lv, positions_next, jnp.broadcast_to(tally, lv.shape)], axis=3
    )
    below = shifted(state[-1:], "gx", 1)
    above = shifted(state[:1], "gx", -1)
    state = jnp.concatenate([below, state, above], axis=0)
    below = shifted(state[:, -1:], "gy", 1)
    above = shifted(state[:, :1], "gy", -1)
    state = jnp.concatenate([below, state, above], axis=1)
    if lax.axis_size("gz") == 2 and cz == 1:
        below = above = shifted(state, "gz", 1)
    else:
        below = shifted(state[:, :, -1:], "gz", 1)
        above = shifted(state[:, :, :1], "gz", -1)
    padded = jnp.concatenate([below, state, above], axis=2).reshape(-1, 8, slots)
    count = padded.shape[0]
    drift, squared, stats = pl.pallas_call(
        functools.partial(kernel, (cx, cy, cz), width),
        out_shape=(
            jax.ShapeDtypeStruct((cells, 3, slots), jnp.float32),
            jax.ShapeDtypeStruct((cells, slots), jnp.float32),
            jax.ShapeDtypeStruct((2, slots), jnp.float32),
        ),
        in_specs=[pl.BlockSpec(memory_space=pltpu.SMEM)] + [pl.BlockSpec(memory_space=pltpu.VMEM)] * 3,
        out_specs=(pl.BlockSpec(memory_space=pltpu.VMEM),) * 3,
        scratch_shapes=[
            pltpu.VMEM((count, 8, slots), jnp.float32),
            pltpu.VMEM((width + SPAN + 1, 8, slots), jnp.float32),
            pltpu.SMEM((count,), jnp.int32),
        ],
    )(
        neighbour_lists.reshape(-1),
        padded,
        velocities.reshape(cells, 3, slots),
        descendants.reshape(cells, 2, slots),
    )
    axes = ("gx", "gy", "gz")
    sizes = tuple(lax.axis_size(name) for name in axes)
    peers = sizes[0] * sizes[1] * sizes[2] - 1
    tension = pl.pallas_call(
        functools.partial(scale_kernel, axes, sizes),
        out_shape=jax.ShapeDtypeStruct((cells, slots), jnp.float32),
        in_specs=[pl.BlockSpec(memory_space=pltpu.VMEM)] * 2,
        out_specs=pl.BlockSpec(memory_space=pltpu.VMEM),
        scratch_shapes=[
            pltpu.VMEM((peers, 2, slots), jnp.float32),
            pltpu.SemaphoreType.DMA,
            pltpu.SemaphoreType.DMA,
        ],
        compiler_params=pltpu.CompilerParams(collective_id=0, has_side_effects=True),
    )(stats, squared)
    return (drift.reshape(cx, cy, cz, 3, slots), tension.reshape(cx, cy, cz, slots))


def solution(mesh):
    return jax.shard_map(
        shards,
        mesh=mesh,
        in_specs=(
            P("gx", "gy", "gz", None, None),
            P("gx", "gy", "gz", None, None),
            P("gx", "gy", "gz", None, None),
            P("gx", "gy", "gz"),
            P("gx", "gy", "gz", None),
            P("gx", "gy", "gz", None, None),
        ),
        out_specs=(P("gx", "gy", "gz", None, None), P("gx", "gy", "gz", None)),
        check_vma=False,
    )
```

profile of v0, /device:TPU:0, one launch (start us, length us, event | category | flops | bytes accessed | tf_op | source)
XLA Modules:
  0.0 77.2 jit_solution(10936351248758235536)
XLA Ops:
  0.6 0.0 copy-start.4
  0.6 0.8 %copy.16 = s32[8,4]{1,0:T(8,128)S(1)} copy(s32[8,4]{0,1:T(4,128)} %bitcast.16) | data formatting | bytes 256 | tf_op jit(solution)/shard_map/lt | solution.py:181
  1.5 0.0 copy-done.4
  1.5 0.8 %slice.24 = f32[8,4,1,3,128]{4,2,3,1,0:T(1,128)S(1)} slice(f32[8,4,1,4,128]{4,2,3,1,0:T(1,128)} %bitcast.12), slice={[0:8], [0:4], [0:1], [0:3], [0:128]} | slice | bytes 98304 | tf_op jit(solution)/shard_map/slice | solution.py:186
  2.3 0.0 copy-start
  2.3 0.8 %compare_select_fusion = f32[8,4,1,1,128]{4,2,3,1,0:T(1,128)S(1)} fusion(f32[8,4,1,4,128]{4,2,3,1,0:T(1,128)} %bitcast.13, s32[8,4]{1,0:T(8,128)S(1)} %copy.16), kind=kLoop, calls=%fused_computation.2 | loop fusion | flops 8192 | bytes 32896 | tf_op jit(solution)/shard_map/mul | solution.py:186
  3.1 0.1 copy.18
  3.2 0.1 broadcast_in_dim.2
  3.3 0.0 copy-done
  3.4 3.1 %collective-permute-start = (f32[1,4,1,8,128]{4,2,3,1,0:T(1,128)S(1)}, f32[1,4,1,8,128]{4,2,3,1,0:T(1,128)S(1)}, u32[]{:S(2)}, u32[]{:S(2)}) collective-permute-start(f32[1,4,1,8,128]{4,2,3,1,0:T(1,128)S(1)} %get-tuple-element.14), channel_id=1, source_target_pairs={{0,8},{8,16},{16,24},{24,0},{1,9},{9,17},{17,25},{25,1},{2,10},{10... | collective-permute-start | bytes 49160 | tf_op jit(solution)/shard_map/ppermute | solution.py:18
  6.5 2.1 %collective-permute-start.1 = (f32[1,4,1,8,128]{4,2,3,1,0:T(1,128)S(1)}, f32[1,4,1,8,128]{4,2,3,1,0:T(1,128)S(1)}, u32[]{:S(2)}, u32[]{:S(2)}) collective-permute-start(f32[1,4,1,8,128]{4,2,3,1,0:T(1,128)S(1)} %get-tuple-element.15), channel_id=1, source_target_pairs={{0,24},{8,0},{16,8},{24,16},{1,25},{9,1},{17,9},{25,17},{2,26},{10... | collective-permute-start | bytes 49160 | tf_op jit(solution)/shard_map/ppermute | solution.py:18
  8.6 1.8 %collective-permute-done = f32[1,4,1,8,128]{4,2,3,1,0:T(1,128)S(1)} collective-permute-done((f32[1,4,1,8,128]{4,2,3,1,0:T(1,128)S(1)}, f32[1,4,1,8,128]{4,2,3,1,0:T(1,128)S(1)}, u32[]{:S(2)}, u32[]{:S(2)}) %collective-permute-start) | collective-permute-done | bytes 16416 | tf_op jit(solution)/shard_map/ppermute | solution.py:18
  10.3 0.1 collective-permute-done.1
  10.4 0.1 pad_maximum_fusion.7
  10.5 0.1 collective-permute-start.2
  10.5 0.0 copy-start.2
  10.5 1.7 %collective-permute-start.3 = (f32[10,1,1,8,128]{4,2,3,1,0:T(1,128)S(1)}, f32[10,1,1,8,128]{4,2,3,1,0:T(1,128)S(1)}, u32[]{:S(2)}, u32[]{:S(2)}) collective-permute-start(f32[10,1,1,8,128]{4,2,3,1,0:T(1,128)S(1)} %get-tuple-element.13), channel_id=1, source_target_pairs={{0,6},{2,0},{4,2},{6,4},{1,7},{3,1},{5,3},{7,5},{8,14},{10,8},{12,... | collective-permute-start | bytes 122888 | tf_op jit(solution)/shard_map/ppermute | solution.py:18
  12.3 1.7 %collective-permute-done.2 = f32[10,1,1,8,128]{4,2,3,1,0:T(1,128)S(1)} collective-permute-done((f32[10,1,1,8,128]{4,2,3,1,0:T(1,128)S(1)}, f32[10,1,1,8,128]{4,2,3,1,0:T(1,128)S(1)}, u32[]{:S(2)}, u32[]{:S(2)}) %collective-permute-start.2) | collective-permute-done | bytes 40992 | tf_op jit(solution)/shard_map/ppermute | solution.py:18
  13.9 0.0 collective-permute-done.3
  13.9 0.2 pad_maximum_fusion.1
  14.2 1.6 %collective-permute-start.4 = (f32[10,6,1,8,128]{4,2,3,1,0:T(1,128)S(1)}, f32[10,6,1,8,128]{4,2,3,1,0:T(1,128)S(1)}, u32[]{:S(2)}, u32[]{:S(2)}) collective-permute-start(f32[10,6,1,8,128]{4,2,3,1,0:T(1,128)S(1)} %pad_maximum_fusion.1), channel_id=1, source_target_pairs={{0,1},{1,0},{2,3},{3,2},{4,5},{5,4},{6,7},{7,6},{8,9},{9,8},{10,11... | collective-permute-start | bytes 737288 | tf_op jit(solution)/shard_map/ppermute | solution.py:18
  15.8 0.0 copy-done.2
  15.8 0.0 copy-start.3
  15.8 0.7 copy.21.vel
  16.5 0.5 broadcast.23
  17.0 0.0 copy-done.3
  17.0 0.7 reduce.3
  17.7 0.7 reshape.43.lists
  18.4 4.0 %collective-permute-done.4 = f32[10,6,1,8,128]{4,2,3,1,0:T(1,128)S(1)} collective-permute-done((f32[10,6,1,8,128]{4,2,3,1,0:T(1,128)S(1)}, f32[10,6,1,8,128]{4,2,3,1,0:T(1,128)S(1)}, u32[]{:S(2)}, u32[]{:S(2)}) %collective-permute-start.4) | collective-permute-done | bytes 245792 | tf_op jit(solution)/shard_map/ppermute | solution.py:18
  22.4 0.6 pad_maximum_fusion
  22.9 0.9 %copy.19 = f32[10,6,3,8,128]{4,3,2,1,0:T(8,128)} copy(f32[10,6,3,8,128]{4,2,3,1,0:T(4,128)S(1)} %pad_maximum_fusion) | data formatting | bytes 1474560 | tf_op jit(solution)/shard_map/concatenate | solution.py:199
  23.9 28.4 %shard_map.77 = (f32[32,3,128]{2,1,0:T(4,128)}, f32[32,128]{1,0:T(8,128)}, f32[2,128]{1,0:T(2,128)}) custom-call(s32[448]{0:T(512)} %reshape.43.lists, f32[180,8,128]{2,1,0:T(8,128)} %bitcast.9, f32[32,3,128]{2,1,0:T(4,128)} %copy.21.vel, s32[32,2,128]{2,1,0:T(2,128)} %bitcast.15), custom_call_target="tpu_custom_call" | custom-call | tf_op jit(solution)/shard_map/pallas_call | solution.py:201
  52.3 22.7 %shard_map.78 = f32[32,128]{1,0:T(8,128)} custom-call(f32[2,128]{1,0:T(2,128)} %get-tuple-element.6.stat, f32[32,128]{1,0:T(8,128)} %get-tuple-element.7.squared), custom_call_target="tpu_custom_call" | custom-call | tf_op jit(solution)/shard_map/pallas_call | solution.py:224
  75.0 0.0 copy-start.1
  75.0 1.5 %copy.22 = f32[8,4,1,3,128]{4,2,3,1,0:T(1,128)} copy(f32[8,4,1,3,128]{4,3,1,0,2:T(4,128)} %bitcast.11) | data formatting | bytes 98304
  76.6 0.0 copy-done.1
  76.6 0.6 copy.25
  (3 shorter events, 0.0 us)
Async XLA Ops:
  0.6 0.8 %copy-start.4 = (s32[8,4,1]{0,2,1:T(1,128)S(1)}, s32[8,4,1]{0,2,1:T(1,128)}, u32[]{:S(2)}) copy-start(s32[8,4,1]{0,2,1:T(1,128)} %param.9) | copy-start | bytes 388
  2.3 1.0 %copy-start = (f32[8,4,1,3,128]{4,2,3,1,0:T(1,128)S(1)}, f32[8,4,1,3,128]{4,2,3,1,0:T(1,128)}, u32[]{:S(2)}) copy-start(f32[8,4,1,3,128]{4,2,3,1,0:T(1,128)} %param.8) | copy-start | bytes 147460
  3.4 6.9 %collective-permute-start = (f32[1,4,1,8,128]{4,2,3,1,0:T(1,128)S(1)}, f32[1,4,1,8,128]{4,2,3,1,0:T(1,128)S(1)}, u32[]{:S(2)}, u32[]{:S(2)}) collective-permute-start(f32[1,4,1,8,128]{4,2,3,1,0:T(1,128)S(1)} %get-tuple-element.14), channel_id=1, source_target_pairs={{0,8},{8,16},{16,24},{24,0},{1,9},{9,17},{17,25},{25,1},{2,10},{10... | collective-permute-start | bytes 49160 | tf_op jit(solution)/shard_map/ppermute | solution.py:18
  6.5 3.9 %collective-permute-start.1 = (f32[1,4,1,8,128]{4,2,3,1,0:T(1,128)S(1)}, f32[1,4,1,8,128]{4,2,3,1,0:T(1,128)S(1)}, u32[]{:S(2)}, u32[]{:S(2)}) collective-permute-start(f32[1,4,1,8,128]{4,2,3,1,0:T(1,128)S(1)} %get-tuple-element.15), channel_id=1, source_target_pairs={{0,24},{8,0},{16,8},{24,16},{1,25},{9,1},{17,9},{25,17},{2,26},{10... | collective-permute-start | bytes 49160 | tf_op jit(solution)/shard_map/ppermute | solution.py:18
  10.5 3.5 %collective-permute-start.2 = (f32[10,1,1,8,128]{4,2,3,1,0:T(1,128)S(1)}, f32[10,1,1,8,128]{4,2,3,1,0:T(1,128)S(1)}, u32[]{:S(2)}, u32[]{:S(2)}) collective-permute-start(f32[10,1,1,8,128]{4,2,3,1,0:T(1,128)S(1)} %get-tuple-element.12), channel_id=1, source_target_pairs={{0,2},{2,4},{4,6},{6,0},{1,3},{3,5},{5,7},{7,1},{8,10},{10,12},{12... | collective-permute-start | bytes 122888 | tf_op jit(solution)/shard_map/ppermute | solution.py:18
  10.5 5.3 %copy-start.2 = (f32[8,4,1,3,128]{4,2,3,1,0:T(1,128)S(1)}, f32[8,4,1,3,128]{4,2,3,1,0:T(1,128)}, u32[]{:S(2)}) copy-start(f32[8,4,1,3,128]{4,2,3,1,0:T(1,128)} %param.7) | copy-start | bytes 147460
  10.5 3.4 %collective-permute-start.3 = (f32[10,1,1,8,128]{4,2,3,1,0:T(1,128)S(1)}, f32[10,1,1,8,128]{4,2,3,1,0:T(1,128)S(1)}, u32[]{:S(2)}, u32[]{:S(2)}) collective-permute-start(f32[10,1,1,8,128]{4,2,3,1,0:T(1,128)S(1)} %get-tuple-element.13), channel_id=1, source_target_pairs={{0,6},{2,0},{4,2},{6,4},{1,7},{3,1},{5,3},{7,5},{8,14},{10,8},{12,... | collective-permute-start | bytes 122888 | tf_op jit(solution)/shard_map/ppermute | solution.py:18
  14.2 8.2 %collective-permute-start.4 = (f32[10,6,1,8,128]{4,2,3,1,0:T(1,128)S(1)}, f32[10,6,1,8,128]{4,2,3,1,0:T(1,128)S(1)}, u32[]{:S(2)}, u32[]{:S(2)}) collective-permute-start(f32[10,6,1,8,128]{4,2,3,1,0:T(1,128)S(1)} %pad_maximum_fusion.1), channel_id=1, source_target_pairs={{0,1},{1,0},{2,3},{3,2},{4,5},{5,4},{6,7},{7,6},{8,9},{9,8},{10,11... | collective-permute-start | bytes 737288 | tf_op jit(solution)/shard_map/ppermute | solution.py:18
  15.8 1.2 %copy-start.3 = (s32[8,4,1,14]{3,2,1,0:T(1,128)S(1)}, s32[8,4,1,14]{3,2,1,0:T(1,128)}, u32[]{:S(2)}) copy-start(s32[8,4,1,14]{3,2,1,0:T(1,128)} %param.10) | copy-start | bytes 5380
  75.0 1.5 %copy-start.1 = (f32[32,128]{1,0:T(8,128)S(1)}, f32[32,128]{1,0:T(8,128)}, u32[]{:S(2)}) copy-start(f32[32,128]{1,0:T(8,128)} %shard_map.78) | copy-start | bytes 49156
where the time goes:
time: 78 us; the launch traced here: 77.2 us
  Pallas kernels  51.2 us (66%)
  starting transfers between devices  8.58 us (11%)
  waiting for transfers between devices  7.47 us (10%)
  local copies, waits for them, and re-layouts  6.78 us (9%)
  other arithmetic  2.43 us (3%)
    pallas_call x1, Pallas kernels, shards(): pl.pallas_call(functools.partial(kernel, (cx, cy, cz), width), out_shape=...  28.4 us
    pallas_call x1, Pallas kernels, shards(): pl.pallas_call(functools.partial(scale_kernel, axes, sizes), out_shape=ja...  22.7 us
    ppermute x5, starting transfers between devices, shifted(): lax.ppermute(shard, axis, [(i, (i + by) % peers) for i in range(peers)])  8.58 us
    ppermute x5, waiting for transfers between devices, shifted(): lax.ppermute(shard, axis, [(i, (i + by) % peers) for i in range(peers)])  7.47 us
    unnamed x14, local copies, waits for them, and re-layouts  2.67 us
  transfers between devices with their start and end apart: 5, of which 4 were waited for; matrix products, arithmetic and copies ran while one was open for 3% of the time, Pallas kernels for 0%

commit v1 on v0

v1 whole, which is shorter than its diff:
```python
import functools

import jax
import jax.numpy as jnp
from jax import lax
from jax.experimental import pallas as pl
from jax.experimental.pallas import tpu as pltpu
from jax.sharding import PartitionSpec as P

EPS_SQ = 0.01
STEP_DT = 0.3
HALF_KICK = 0.045
AXES = ("gx", "gy", "gz")
GROUP = 4
MESH = pl.DeviceIdType.MESH


def pieces(tile):
    first = tile.astype(jnp.bfloat16).astype(jnp.float32)
    rest = tile - first
    second = rest.astype(jnp.bfloat16).astype(jnp.float32)
    return first, second, rest - second


def kernel(
    dims, width, sizes, lists, counts, pos_hbm, next_hbm, vel_hbm, desc_hbm, drift_ref, tension_ref,
    pos, nxt, vel, desc, now_pad, next_pad, feats, moms, lhs, squared, stat, inbox,
    load_sems, now_send, now_recv, next_send, next_recv, stat_send, stat_recv,
):
    cx, cy, cz = dims
    sx, sy, sz = sizes
    py, pz = cy + 2, cz + 2
    cells = cx * cy * cz
    slots = pos.shape[-1]
    folded = sz == 2 and cz == 1
    total = sx * sy * sz
    me = tuple(lax.axis_index(name) for name in AXES)
    row8 = lax.broadcasted_iota(jnp.int32, (8, slots), 0)
    row4 = lax.broadcasted_iota(jnp.int32, (4, slots), 0)
    lane4 = lax.broadcasted_iota(jnp.int32, (4, slots), 1)

    loads = [
        pltpu.make_async_copy(src, dst, load_sems.at[i])
        for i, (src, dst) in enumerate(((pos_hbm, pos), (next_hbm, nxt), (vel_hbm, vel), (desc_hbm, desc)))
    ]
    for load in loads:
        load.start()

    def peer(step):
        where = []
        at = step
        for mine, size in zip(reversed(me), reversed(sizes)):
            where.append(lax.rem(mine + at % size, size))
            at = at // size
        return tuple(reversed(where))

    def each_peer(act):
        if total <= 64:
            for step in range(1, total):
                act(step, peer(step))
        else:
            lax.fori_loop(1, total, lambda step, _: (act(step, peer(step)), 0)[1], 0)

    barrier = pltpu.get_barrier_semaphore()
    each_peer(lambda step, who: pl.semaphore_signal(barrier, inc=1, device_id=who, device_id_type=MESH))

    def plane(iz, dz):
        return (1 if dz == 0 else 0) if folded else iz + 1 + dz

    def split(n):
        return n // (cy * cz), n // cz % cy, n % cz

    def shift_of(ix, iy, iz):
        fx = ix.astype(jnp.float32) - (cx + 2) / 2
        fy = iy.astype(jnp.float32) - (cy + 2) / 2
        fz = iz.astype(jnp.float32) - (cz + 2) / 2
        return jnp.where(row4 == 0, fx, jnp.where(row4 == 1, fy, jnp.where(row4 == 2, fz, 0.0)))

    loads[0].wait()
    loads[1].wait()

    def stage(n, _):
        ix, iy, iz = split(n)
        tile = pos[n]
        now_pad[ix + 1, iy + 1, plane(iz, 0)] = jnp.where((row4 == 3) & (lane4 >= counts[iy, iz, ix]), 0.0, tile)
        rows = [nxt[pl.ds(3 * n + r, 1), :] for r in range(3)]
        next_pad[ix + 1, iy + 1, plane(iz, 0)] = jnp.concatenate(rows + [jnp.zeros_like(rows[0])], axis=0)
        return 0

    lax.fori_loop(0, cells, stage, 0, unroll=4)

    def face(d, size):
        if d == 0:
            return pl.ds(1, size), pl.ds(1, size)
        return (pl.ds(size, 1), pl.ds(0, 1)) if d > 0 else (pl.ds(1, 1), pl.ds(size + 1, 1))

    ways = [
        (dx, dy, dz)
        for dz in ((0, 1) if folded else (0, 1, -1))
        for dx in (0, 1, -1)
        for dy in (0, 1, -1)
        if (dx, dy, dz) != (0, 0, 0)
    ]
    ways.sort(key=lambda way: (way[2] == 0, abs(way[0]) + abs(way[1])))

    def exchange(buf, send_sems, recv_sems):
        made = []
        for i, (dx, dy, dz) in enumerate(ways):
            fx, tx = face(dx, cx)
            fy, ty = face(dy, cy)
            if folded:
                fz, tz = pl.ds(1, 1), pl.ds(1 - dz, 1)
            else:
                fz, tz = face(dz, cz)
            who = tuple(lax.rem(mine + d + size, size) for mine, d, size in zip(me, (dx, dy, dz), sizes))
            made.append(
                pltpu.make_async_remote_copy(
                    src_ref=buf.at[fx, fy, fz],
                    dst_ref=buf.at[tx, ty, tz],
                    send_sem=send_sems.at[i],
                    recv_sem=recv_sems.at[i],
                    device_id=who,
                    device_id_type=MESH,
                )
            )
        for copy in made:
            copy.start()
        return made

    pl.semaphore_wait(barrier, total - 1)
    now_copies = exchange(now_pad, now_send, now_recv)
    next_copies = exchange(next_pad, next_send, next_recv)

    def prepare(px, py_, image, at_plane):
        tile = now_pad[px, py_, at_plane]
        spot = tile + shift_of(jnp.int32(px), jnp.int32(py_), jnp.int32(image))
        square = spot * spot
        size = square[0:1] + square[1:2] + square[2:3]
        base = jnp.where(row4 == 3, size, spot)
        full = jnp.concatenate([base, jnp.where(row4 == 0, 1.0, 0.0)], axis=0)
        a, b, c = pieces(full)
        index = (px * py + py_) * pz + image
        feats[index] = jnp.concatenate([a, a, a, b, b, c], axis=0).astype(jnp.bfloat16)
        mass = tile[3:4]
        mom = jnp.where(row4 == 3, mass, spot * mass)
        mom = jnp.concatenate([mom, jnp.zeros_like(mom)], axis=0)
        high = mom.astype(jnp.bfloat16).astype(jnp.float32)
        moms[index] = jnp.concatenate([high, mom - high], axis=0).astype(jnp.bfloat16)
        return spot, size

    def mine(n, _):
        ix, iy, iz = split(n)
        spot, size = prepare(ix + 1, iy + 1, iz + 1, plane(iz, 0))
        base = jnp.where(row4 == 3, 1.0, -2.0 * spot)
        extra = jnp.where(row4 == 0, size + EPS_SQ, 0.0)
        a, b, c = pieces(jnp.concatenate([base, extra], axis=0))
        lhs[n] = jnp.concatenate([a, b, c, a, b, a], axis=0).T.astype(jnp.bfloat16)
        return 0

    lax.fori_loop(0, cells, mine, 0, unroll=4)
    for copy in now_copies:
        copy.wait()

    def rim_x(i, _):
        for px in (0, cx + 1):
            prepare(px, i // cz, i % cz + 1, plane(i % cz, 0))
        return 0

    def rim_y(i, _):
        for py_ in (0, cy + 1):
            prepare(i // cz + 1, py_, i % cz + 1, plane(i % cz, 0))
        return 0

    def rim_z(i, _):
        for image, dz in ((0, -1), (cz + 1, 1)):
            prepare(i // py, i % py, image, plane(0 if dz < 0 else cz - 1, dz))
        return 0

    lax.fori_loop(0, py * cz, rim_x, 0, unroll=2)
    lax.fori_loop(0, cx * cz, rim_y, 0, unroll=2)
    lax.fori_loop(0, (cx + 2) * py, rim_z, 0, unroll=2)
    for copy in next_copies:
        copy.wait()
    loads[2].wait()
    loads[3].wait()

    def pull(n):
        ix, iy, iz = split(n)
        corner = (ix * py + iy) * pz + iz
        sources = []
        for k in range(width):
            code = lists[n, 0, k]
            d9 = (code * 57) >> 9
            d3 = (code * 43) >> 7
            sources.append(corner + d9 * (py * pz) + (d3 - 3 * d9) * pz + code - 3 * d3)
        own = lhs[n]
        acc = jnp.zeros((16, 2 * slots), jnp.float32)
        for k in range(0, width, 2):
            pair = sources[k : k + 2]
            x = jnp.concatenate([feats[s] for s in pair], axis=1)
            z = jnp.concatenate([moms[s] for s in pair], axis=1)
            inv = lax.rsqrt(jnp.dot(own, x, preferred_element_type=jnp.float32))
            weight = inv * inv * inv
            high = weight.astype(jnp.bfloat16)
            low = (weight - high.astype(jnp.float32)).astype(jnp.bfloat16)
            both = jnp.concatenate([high, low], axis=0)
            acc += lax.dot_general(z, both, (((1,), (1,)), ((), ())), preferred_element_type=jnp.float32)
        acc = acc[:, :slots] + acc[:, slots:]
        return acc[0:4] + acc[8:12]

    def target(n, stats):
        ix, iy, iz = split(n)
        sums = pull(n)
        tile = now_pad[ix + 1, iy + 1, plane(iz, 0)]
        accel = sums - (tile + shift_of(ix + 1, iy + 1, iz + 1)) * sums[3:4]
        rows = [vel[pl.ds(3 * n + r, 1), :] for r in range(3)]
        speed = jnp.concatenate(rows + [jnp.zeros_like(rows[0])], axis=0)
        predicted = tile + STEP_DT * speed + HALF_KICK * accel
        links = desc[n]
        dcode = links[0:1]
        d9 = (dcode * 57) >> 9
        d3 = (dcode * 43) >> 7
        dz = dcode - 3 * d3
        d3 = jnp.broadcast_to(d3, (8, slots))
        dslot = jnp.broadcast_to(links[1:2], (8, slots))
        found = [jnp.zeros((8, slots), jnp.float32)] * (1 if folded else 2)
        for c in range(9):
            at = (ix + c // 3, iy + c % 3)
            tiles = [next_pad[at + (plane(iz, d),)] for d in ((-1, 0) if folded else (-1, 0, 1))]
            if not folded:
                tiles.append(jnp.zeros_like(tiles[0]))
            for h in range(len(tiles) // 2):
                got = jnp.take_along_axis(jnp.concatenate(tiles[2 * h : 2 * h + 2], axis=0), dslot, axis=1)
                found[h] = jnp.where(d3 == c, got, found[h])
        if folded:
            there = jnp.where(dz == 1, found[0][4:8], found[0][0:4])
        else:
            there = jnp.where(dz == 1, found[0][4:8], jnp.where(dz == 0, found[0][0:4], found[1][0:4]))
        step = jnp.where(row4 == 0, d9, jnp.where(row4 == 1, d3[0:4] - 3 * d9, dz)).astype(jnp.float32) - 1.0
        live = lane4 < counts[iy, iz, ix]
        error = jnp.where(live & (row4 < 3), step + there - predicted, 0.0)
        for r in range(3):
            drift_ref[pl.ds(3 * n + r, 1), :] = error[r : r + 1]
        summed = jnp.sum(error * error, axis=0, keepdims=True)
        squared[pl.ds(n, 1), :] = summed
        return stats + jnp.where(row8 == 0, summed, jnp.where((row8 == 1) & live[0:1], 1.0, 0.0))

    group = GROUP if cells % GROUP == 0 else 1

    def several(i, stats):
        for u in range(group):
            stats = target(i * group + u, stats)
        return stats

    stats = lax.fori_loop(0, cells // group, several, jnp.zeros((8, slots), jnp.float32))
    stat[...] = stats[0:2]

    def report(step, who):
        pltpu.make_async_remote_copy(
            src_ref=stat,
            dst_ref=inbox.at[step - 1],
            send_sem=stat_send,
            recv_sem=stat_recv,
            device_id=who,
            device_id_type=MESH,
        ).start()

    each_peer(report)
    pltpu.make_async_copy(inbox, inbox, stat_recv).wait()
    sums = stat[...] + jnp.sum(inbox[...], axis=0)
    mean_sq = jnp.sum(sums[0:1], axis=1, keepdims=True) / jnp.sum(sums[1:2], axis=1, keepdims=True)
    tension_ref[...] = squared[...] / (mean_sq + 1e-06)
    pltpu.make_async_copy(inbox, inbox, stat_send).wait()


def shards(positions_now, velocities, positions_next, halo_counts, neighbour_lists, descendants):
    slots = positions_now.shape[-1]
    cx, cy, cz, width = neighbour_lists.shape
    cells = cx * cy * cz
    sizes = tuple(lax.axis_size(name) for name in AXES)
    folded = sizes[2] == 2 and cz == 1
    planes = 2 if folded else cz + 2
    padded = (cx + 2) * (cy + 2) * (cz + 2)
    ways = 17 if folded else 26
    peers = sizes[0] * sizes[1] * sizes[2] - 1

    def rows(array):
        return jnp.transpose(array, (0, 1, 2, 3, 4)).reshape(cells * 3, slots)

    drift, tension = pl.pallas_call(
        functools.partial(kernel, (cx, cy, cz), width, sizes),
        out_shape=(
            jax.ShapeDtypeStruct((cells * 3, slots), jnp.float32),
            jax.ShapeDtypeStruct((cells, slots), jnp.float32),
        ),
        in_specs=[pl.BlockSpec(memory_space=pltpu.SMEM)] * 2 + [pl.BlockSpec(memory_space=pl.ANY)] * 4,
        out_specs=(pl.BlockSpec(memory_space=pltpu.VMEM),) * 2,
        scratch_shapes=[
            pltpu.VMEM((cells, 4, slots), jnp.float32),
            pltpu.VMEM((cells * 3, slots), jnp.float32),
            pltpu.VMEM((cells * 3, slots), jnp.float32),
            pltpu.VMEM((cells, 2, slots), jnp.int32),
            pltpu.VMEM((cx + 2, cy + 2, planes, 4, slots), jnp.float32),
            pltpu.VMEM((cx + 2, cy + 2, planes, 4, slots), jnp.float32),
            pltpu.VMEM((padded, 48, slots), jnp.bfloat16),
            pltpu.VMEM((padded, 16, slots), jnp.bfloat16),
            pltpu.VMEM((cells, slots, 48), jnp.bfloat16),
            pltpu.VMEM((cells, slots), jnp.float32),
            pltpu.VMEM((2, slots), jnp.float32),
            pltpu.VMEM((peers, 2, slots), jnp.float32),
            pltpu.SemaphoreType.DMA((4,)),
            pltpu.SemaphoreType.DMA((ways,)),
            pltpu.SemaphoreType.DMA((ways,)),
            pltpu.SemaphoreType.DMA((ways,)),
            pltpu.SemaphoreType.DMA((ways,)),
            pltpu.SemaphoreType.DMA,
            pltpu.SemaphoreType.DMA,
        ],
        compiler_params=pltpu.CompilerParams(collective_id=0, has_side_effects=True),
    )(
        neighbour_lists.reshape(cells, 1, width),
        jnp.transpose(halo_counts, (1, 2, 0)),
        positions_now.reshape(cells, 4, slots),
        rows(positions_next),
        rows(velocities),
        descendants.reshape(cells, 2, slots),
    )
    return (drift.reshape(cx, cy, cz, 3, slots), tension.reshape(cx, cy, cz, slots))


def solution(mesh):
    return jax.shard_map(
        shards,
        mesh=mesh,
        in_specs=(
            P("gx", "gy", "gz", None, None),
            P("gx", "gy", "gz", None, None),
            P("gx", "gy", "gz", None, None),
            P("gx", "gy", "gz"),
            P("gx", "gy", "gz", None),
            P("gx", "gy", "gz", None, None),
        ),
        out_specs=(P("gx", "gy", "gz", None, None), P("gx", "gy", "gz", None)),
        check_vma=False,
    )
```

time: 78 us -> 55 us (0.71)
  starting transfers between devices: 8.58 us -> 0 us
  waiting for transfers between devices: 7.47 us -> 0 us
  local copies, waits for them, and re-layouts: 6.78 us -> 2.06 us
  other arithmetic: 2.43 us -> 0 us
  Pallas kernels: 51.2 us -> 52 us
    ppermute x5 -> x0, starting transfers between devices: 8.58 us -> none  [shifted(): lax.ppermute(shard, axis, [(i, (i + by) % peers) for i in range(peers)])]
    ppermute x5 -> x0, waiting for transfers between devices: 7.47 us -> none  [shifted(): lax.ppermute(shard, axis, [(i, (i + by) % peers) for i in range(peers)])]
    reshape x2 -> x0, local copies, waits for them, and re-layouts: 1.36 us -> none  [the longest x1 0.69 us: shards(): neighbour_lists.reshape(-1)]
    concatenate x1 -> x0, local copies, waits for them, and re-layouts: 0.94 us -> none  [shards(): jnp.concatenate([below, state, above], axis=2).reshape(-1, 8, slots)]
    pallas_call x2 -> x1, Pallas kernels: 51.2 us -> 52 us  [shards(): pl.pallas_call(functools.partial(kernel, (cx, cy, cz), width, sizes), out...]
    mul x1 -> x0, other arithmetic: 0.83 us -> none  [shards(): positions_now[:, :, :, 3:4, :] * lv]
    slice x1 -> x0, local copies, waits for them, and re-layouts: 0.82 us -> none  [shards(): positions_now[:, :, :, :3, :]]
    lt x1 -> x0, local copies, waits for them, and re-layouts: 0.82 us -> none  [shards(): jnp.arange(slots, dtype=jnp.int32)[None, None, None, :]]
  transfers between devices with their start and end apart: 5 -> 0, of which waited for: 4 -> 0; matrix products, arithmetic and copies ran while one was open for 3% -> 0% of each run, Pallas kernels for 0% -> 0%
where the time goes in v1:
time: 55 us; the launch traced here: 54.7 us
  Pallas kernels  52 us (95%)
  local copies, waits for them, and re-layouts  2.06 us (4%)
  between operations  0.65 us (1%)
    pallas_call x1, Pallas kernels, shards(): pl.pallas_call(functools.partial(kernel, (cx, cy, cz), width, sizes), out...  52 us
    unnamed x4, local copies, waits for them, and re-layouts  2.06 us

profile of v1, /device:TPU:0, one launch (start us, length us, event | category | flops | bytes accessed | tf_op | source)
XLA Modules:
  0.0 54.7 jit_solution(6309481762130160369)
XLA Ops:
  0.6 52.0 %shard_map.77 = (f32[96,128]{1,0:T(8,128)}, f32[32,128]{1,0:T(8,128)}) custom-call(s32[32,1,14]{2,1,0:T(1,128)} %bitcast.16, s32[4,1,8]{2,1,0:T(1,128)} %bitcast.17, f32[32,4,128]{2,1,0:T(4,128)} %bitcast.10, f32[96,128]{1,0:T(8,128)} %bitcast.12, f32[96,128]{1,0:T(8,128)} %bitcast.13, s32[32,2,128]{2,1,0:T(2,128)} %bitcast.14), custom_call_target="tpu_custom_call" | custom-call | tf_op jit(solution)/shard_map/pallas_call | solution.py:290
  52.7 0.0 copy-start
  52.7 1.4 %copy.14 = f32[8,4,1,3,128]{4,2,3,1,0:T(1,128)} copy(f32[8,4,1,3,128]{4,2,3,1,0:T(1,128)} %bitcast.11) | data formatting | bytes 98304
  54.1 0.0 copy-done
  54.1 0.6 %copy.15 = f32[8,4,1,128]{3,2,1,0:T(1,128)} copy(f32[8,4,1,128]{3,2,1,0:T(1,128)S(1)} %bitcast.15) | data formatting | bytes 32768
Async XLA Ops:
  52.7 1.5 %copy-start = (f32[32,128]{1,0:T(8,128)S(1)}, f32[32,128]{1,0:T(8,128)}, u32[]{:S(2)}) copy-start(f32[32,128]{1,0:T(8,128)} %get-tuple-element.5) | copy-start | bytes 49156

commit v2 on v1

--- a/solution.py
+++ b/solution.py
@@ -11,7 +11,8 @@
 STEP_DT = 0.3
 HALF_KICK = 0.045
 AXES = ("gx", "gy", "gz")
-GROUP = 4
+GROUP = 8
+ROWS = 32
 MESH = pl.DeviceIdType.MESH
 
 
@@ -131,16 +132,18 @@
     now_copies = exchange(now_pad, now_send, now_recv)
     next_copies = exchange(next_pad, next_send, next_recv)
 
+    units = jnp.where(row8 < 3, 1.0, 0.0)
+
     def prepare(px, py_, image, at_plane):
         tile = now_pad[px, py_, at_plane]
         spot = tile + shift_of(jnp.int32(px), jnp.int32(py_), jnp.int32(image))
         square = spot * spot
         size = square[0:1] + square[1:2] + square[2:3]
         base = jnp.where(row4 == 3, size, spot)
-        full = jnp.concatenate([base, jnp.where(row4 == 0, 1.0, 0.0)], axis=0)
-        a, b, c = pieces(full)
+        a, b, c = pieces(jnp.concatenate([base, base], axis=0))
         index = (px * py + py_) * pz + image
-        feats[index] = jnp.concatenate([a, a, a, b, b, c], axis=0).astype(jnp.bfloat16)
+        rows = jnp.concatenate([a, jnp.where(row8 < 4, a, b), jnp.where(row8 < 4, b, c), units], axis=0)
+        feats[index, :, 0:ROWS] = rows.astype(jnp.bfloat16).T
         mass = tile[3:4]
         mom = jnp.where(row4 == 3, mass, spot * mass)
         mom = jnp.concatenate([mom, jnp.zeros_like(mom)], axis=0)
@@ -152,11 +155,18 @@
         ix, iy, iz = split(n)
         spot, size = prepare(ix + 1, iy + 1, iz + 1, plane(iz, 0))
         base = jnp.where(row4 == 3, 1.0, -2.0 * spot)
-        extra = jnp.where(row4 == 0, size + EPS_SQ, 0.0)
-        a, b, c = pieces(jnp.concatenate([base, extra], axis=0))
-        lhs[n] = jnp.concatenate([a, b, c, a, b, a], axis=0).T.astype(jnp.bfloat16)
-        return 0
-
+        a, b, c = pieces(jnp.concatenate([base, base], axis=0))
+        n1, n2, n3 = pieces(jnp.broadcast_to(size + EPS_SQ, (8, slots)))
+        norm = jnp.where(row8 == 0, n1, jnp.where(row8 == 1, n2, jnp.where(row8 == 2, n3, 0.0)))
+        rows = jnp.concatenate([jnp.where(row8 < 4, a, b), jnp.where(row8 < 4, c, a), jnp.where(row8 < 4, b, a), norm], axis=0)
+        lhs[n] = rows.astype(jnp.bfloat16)
+        return 0
+
+    def clear(i, _):
+        feats[i] = jnp.zeros((slots, slots), jnp.bfloat16)
+        return 0
+
+    lax.fori_loop(0, feats.shape[0], clear, 0, unroll=6)
     lax.fori_loop(0, cells, mine, 0, unroll=4)
     for copy in now_copies:
         copy.wait()
@@ -187,24 +197,32 @@
     def pull(n):
         ix, iy, iz = split(n)
         corner = (ix * py + iy) * pz + iz
+        own = lhs[n]
+        blank = jnp.zeros((slots - ROWS, slots), jnp.bfloat16)
+        own = jnp.concatenate([own, blank], axis=0)
+        none = jnp.zeros_like(own)
+        both = jnp.concatenate(
+            [jnp.concatenate([own, none], axis=1), jnp.concatenate([none, own], axis=1)], axis=0
+        )
         sources = []
         for k in range(width):
             code = lists[n, 0, k]
             d9 = (code * 57) >> 9
             d3 = (code * 43) >> 7
             sources.append(corner + d9 * (py * pz) + (d3 - 3 * d9) * pz + code - 3 * d3)
-        own = lhs[n]
         acc = jnp.zeros((16, 2 * slots), jnp.float32)
         for k in range(0, width, 2):
             pair = sources[k : k + 2]
             x = jnp.concatenate([feats[s] for s in pair], axis=1)
             z = jnp.concatenate([moms[s] for s in pair], axis=1)
-            inv = lax.rsqrt(jnp.dot(own, x, preferred_element_type=jnp.float32))
+            inv = lax.rsqrt(jnp.dot(x, both, preferred_element_type=jnp.float32))
             weight = inv * inv * inv
             high = weight.astype(jnp.bfloat16)
             low = (weight - high.astype(jnp.float32)).astype(jnp.bfloat16)
-            both = jnp.concatenate([high, low], axis=0)
-            acc += lax.dot_general(z, both, (((1,), (1,)), ((), ())), preferred_element_type=jnp.float32)
+            w = jnp.concatenate(
+                [jnp.concatenate([high[:, h * slots : (h + 1) * slots], low[:, h * slots : (h + 1) * slots]], axis=1) for h in range(2)], axis=0
+            )
+            acc += jnp.dot(z, w, preferred_element_type=jnp.float32)
         acc = acc[:, :slots] + acc[:, slots:]
         return acc[0:4] + acc[8:12]
 
@@ -302,9 +320,9 @@
             pltpu.VMEM((cells, 2, slots), jnp.int32),
             pltpu.VMEM((cx + 2, cy + 2, planes, 4, slots), jnp.float32),
             pltpu.VMEM((cx + 2, cy + 2, planes, 4, slots), jnp.float32),
-            pltpu.VMEM((padded, 48, slots), jnp.bfloat16),
+            pltpu.VMEM((padded, slots, slots), jnp.bfloat16),
             pltpu.VMEM((padded, 16, slots), jnp.bfloat16),
-            pltpu.VMEM((cells, slots, 48), jnp.bfloat16),
+            pltpu.VMEM((cells, ROWS, slots), jnp.bfloat16),
             pltpu.VMEM((cells, slots), jnp.float32),
             pltpu.VMEM((2, slots), jnp.float32),
             pltpu.VMEM((peers, 2, slots), jnp.float32),

time: 55 us -> 34.1 us (0.62)
  Pallas kernels: 52 us -> 31.1 us
    pallas_call x1, Pallas kernels: 52 us -> 31.1 us  [shards(): pl.pallas_call(functools.partial(kernel, (cx, cy, cz), width, sizes), out...]
where the time goes in v2:
time: 34.1 us; the launch traced here: 33.8 us
  Pallas kernels  31.1 us (91%)
  local copies, waits for them, and re-layouts  2.06 us (6%)
  between operations  0.65 us (2%)
    pallas_call x1, Pallas kernels, shards(): pl.pallas_call(functools.partial(kernel, (cx, cy, cz), width, sizes), out...  31.1 us
    unnamed x4, local copies, waits for them, and re-layouts  2.06 us

profile of v2, /device:TPU:0, one launch (start us, length us, event | category | flops | bytes accessed | tf_op | source)
XLA Modules:
  0.0 33.8 jit_solution(12776795019583306592)
XLA Ops:
  0.6 31.1 %shard_map.77 = (f32[96,128]{1,0:T(8,128)}, f32[32,128]{1,0:T(8,128)}) custom-call(s32[32,1,14]{2,1,0:T(1,128)} %bitcast.16, s32[4,1,8]{2,1,0:T(1,128)} %bitcast.17, f32[32,4,128]{2,1,0:T(4,128)} %bitcast.10, f32[96,128]{1,0:T(8,128)} %bitcast.12, f32[96,128]{1,0:T(8,128)} %bitcast.13, s32[32,2,128]{2,1,0:T(2,128)} %bitcast.14), custom_call_target="tpu_custom_call" | custom-call | tf_op jit(solution)/shard_map/pallas_call | solution.py:308
  31.7 0.0 copy-start
  31.8 1.4 %copy.14 = f32[8,4,1,3,128]{4,2,3,1,0:T(1,128)} copy(f32[8,4,1,3,128]{4,2,3,1,0:T(1,128)} %bitcast.11) | data formatting | bytes 98304
  33.2 0.0 copy-done
  33.2 0.6 %copy.15 = f32[8,4,1,128]{3,2,1,0:T(1,128)} copy(f32[8,4,1,128]{3,2,1,0:T(1,128)S(1)} %bitcast.15) | data formatting | bytes 32768
Async XLA Ops:
  31.7 1.5 %copy-start = (f32[32,128]{1,0:T(8,128)S(1)}, f32[32,128]{1,0:T(8,128)}, u32[]{:S(2)}) copy-start(f32[32,128]{1,0:T(8,128)} %get-tuple-element.5) | copy-start | bytes 49156

commit v3 on v2

--- a/solution.py
+++ b/solution.py
@@ -11,7 +11,7 @@
 STEP_DT = 0.3
 HALF_KICK = 0.045
 AXES = ("gx", "gy", "gz")
-GROUP = 8
+GROUP = 16
 ROWS = 32
 MESH = pl.DeviceIdType.MESH
 
@@ -24,9 +24,9 @@
 
 
 def kernel(
-    dims, width, sizes, lists, counts, pos_hbm, next_hbm, vel_hbm, desc_hbm, drift_ref, tension_ref,
-    pos, nxt, vel, desc, now_pad, next_pad, feats, moms, lhs, squared, stat, inbox,
-    load_sems, now_send, now_recv, next_send, next_recv, stat_send, stat_recv,
+    dims, width, sizes, lists_hbm, counts_hbm, pos_hbm, next_hbm, vel_hbm, desc_hbm, ends_hbm, tension_hbm,
+    lists, counts, pos, nxt, vel, desc, now_pad, next_pad, feats, moms, lhs, ends, squared, tension, stat, inbox,
+    load_sems, end_sem, now_send, now_recv, next_send, next_recv, stat_send, stat_recv,
 ):
     cx, cy, cz = dims
     sx, sy, sz = sizes
@@ -42,7 +42,9 @@
 
     loads = [
         pltpu.make_async_copy(src, dst, load_sems.at[i])
-        for i, (src, dst) in enumerate(((pos_hbm, pos), (next_hbm, nxt), (vel_hbm, vel), (desc_hbm, desc)))
+        for i, (src, dst) in enumerate(
+            ((counts_hbm, counts), (pos_hbm, pos), (next_hbm, nxt), (lists_hbm, lists), (vel_hbm, vel), (desc_hbm, desc))
+        )
     ]
     for load in loads:
         load.start()
@@ -55,9 +57,14 @@
             at = at // size
         return tuple(reversed(where))
 
-    def each_peer(act):
+    def far(step):
+        gaps = (step // (sy * sz), step // sz % sy, step % sz)
+        near = [min(gap, size - gap) for gap, size in zip(gaps, sizes)]
+        return max(near) > 1, sum(near)
+
+    def each_peer(act, outward=True):
         if total <= 64:
-            for step in range(1, total):
+            for step in sorted(range(1, total), key=far, reverse=not outward):
                 act(step, peer(step))
         else:
             lax.fori_loop(1, total, lambda step, _: (act(step, peer(step)), 0)[1], 0)
@@ -77,18 +84,16 @@
         fz = iz.astype(jnp.float32) - (cz + 2) / 2
         return jnp.where(row4 == 0, fx, jnp.where(row4 == 1, fy, jnp.where(row4 == 2, fz, 0.0)))
 
-    loads[0].wait()
-    loads[1].wait()
-
-    def stage(n, _):
-        ix, iy, iz = split(n)
-        tile = pos[n]
-        now_pad[ix + 1, iy + 1, plane(iz, 0)] = jnp.where((row4 == 3) & (lane4 >= counts[iy, iz, ix]), 0.0, tile)
+    def stage_now(n, _):
+        ix, iy, iz = split(n)
+        now_pad[ix + 1, iy + 1, plane(iz, 0)] = jnp.where((row4 == 3) & (lane4 >= counts[iy, iz, ix]), 0.0, pos[n])
+        return 0
+
+    def stage_next(n, _):
+        ix, iy, iz = split(n)
         rows = [nxt[pl.ds(3 * n + r, 1), :] for r in range(3)]
         next_pad[ix + 1, iy + 1, plane(iz, 0)] = jnp.concatenate(rows + [jnp.zeros_like(rows[0])], axis=0)
         return 0
-
-    lax.fori_loop(0, cells, stage, 0, unroll=4)
 
     def face(d, size):
         if d == 0:
@@ -102,7 +107,7 @@
         for dy in (0, 1, -1)
         if (dx, dy, dz) != (0, 0, 0)
     ]
-    ways.sort(key=lambda way: (way[2] == 0, abs(way[0]) + abs(way[1])))
+    ways.sort(key=lambda way: ((way[0], way[1]) != (0, 0), way[2] != 0, abs(way[0]) + abs(way[1])))
 
     def exchange(buf, send_sems, recv_sems):
         made = []
@@ -128,8 +133,13 @@
             copy.start()
         return made
 
+    loads[0].wait()
+    loads[1].wait()
+    lax.fori_loop(0, cells, stage_now, 0, unroll=8)
     pl.semaphore_wait(barrier, total - 1)
     now_copies = exchange(now_pad, now_send, now_recv)
+    loads[2].wait()
+    lax.fori_loop(0, cells, stage_next, 0, unroll=8)
     next_copies = exchange(next_pad, next_send, next_recv)
 
     units = jnp.where(row8 < 3, 1.0, 0.0)
@@ -143,7 +153,8 @@
         a, b, c = pieces(jnp.concatenate([base, base], axis=0))
         index = (px * py + py_) * pz + image
         rows = jnp.concatenate([a, jnp.where(row8 < 4, a, b), jnp.where(row8 < 4, b, c), units], axis=0)
-        feats[index, :, 0:ROWS] = rows.astype(jnp.bfloat16).T
+        rows = rows.astype(jnp.bfloat16)
+        feats[index, :, 0 : 2 * ROWS] = jnp.concatenate([rows, rows], axis=0).T
         mass = tile[3:4]
         mom = jnp.where(row4 == 3, mass, spot * mass)
         mom = jnp.concatenate([mom, jnp.zeros_like(mom)], axis=0)
@@ -162,44 +173,47 @@
         lhs[n] = rows.astype(jnp.bfloat16)
         return 0
 
-    def clear(i, _):
-        feats[i] = jnp.zeros((slots, slots), jnp.bfloat16)
-        return 0
-
-    lax.fori_loop(0, feats.shape[0], clear, 0, unroll=6)
-    lax.fori_loop(0, cells, mine, 0, unroll=4)
-    for copy in now_copies:
-        copy.wait()
-
-    def rim_x(i, _):
+    lax.fori_loop(0, cells, mine, 0, unroll=8)
+
+    def settle(pick):
+        for way, copy in zip(ways, now_copies):
+            if pick(*way):
+                copy.wait()
+
+    def over(length, body):
+        lax.fori_loop(0, length, lambda i, _: (body(i), 0)[1], 0, unroll=True if length <= 8 else 4)
+
+    def both_images(px, py_):
+        for image, iz, dz in ((0, 0, -1), (cz + 1, cz - 1, 1)):
+            prepare(px, py_, image, plane(iz, dz))
+
+    def rim_x(i):
         for px in (0, cx + 1):
             prepare(px, i // cz, i % cz + 1, plane(i % cz, 0))
-        return 0
-
-    def rim_y(i, _):
+
+    def rim_y(i):
         for py_ in (0, cy + 1):
             prepare(i // cz + 1, py_, i % cz + 1, plane(i % cz, 0))
-        return 0
-
-    def rim_z(i, _):
-        for image, dz in ((0, -1), (cz + 1, 1)):
-            prepare(i // py, i % py, image, plane(0 if dz < 0 else cz - 1, dz))
-        return 0
-
-    lax.fori_loop(0, py * cz, rim_x, 0, unroll=2)
-    lax.fori_loop(0, cx * cz, rim_y, 0, unroll=2)
-    lax.fori_loop(0, (cx + 2) * py, rim_z, 0, unroll=2)
+
+    settle(lambda dx, dy, dz: dz == 0)
+    over(py * cz, rim_x)
+    over(cx * cz, rim_y)
+    settle(lambda dx, dy, dz: dz != 0 and dx == 0 and dy == 0)
+    over(cx * cy, lambda i: both_images(i // cy + 1, i % cy + 1))
+    settle(lambda dx, dy, dz: dz != 0 and (dx != 0 or dy != 0))
+    over(py, lambda i: [both_images(px, i) for px in (0, cx + 1)])
+    over(cx, lambda i: [both_images(i + 1, py_) for py_ in (0, cy + 1)])
     for copy in next_copies:
         copy.wait()
-    loads[2].wait()
-    loads[3].wait()
+    for load in loads[3:]:
+        load.wait()
+
+    first_half = lax.broadcasted_iota(jnp.int32, (slots, 2 * ROWS), 1) < ROWS
 
     def pull(n):
         ix, iy, iz = split(n)
         corner = (ix * py + iy) * pz + iz
         own = lhs[n]
-        blank = jnp.zeros((slots - ROWS, slots), jnp.bfloat16)
-        own = jnp.concatenate([own, blank], axis=0)
         none = jnp.zeros_like(own)
         both = jnp.concatenate(
             [jnp.concatenate([own, none], axis=1), jnp.concatenate([none, own], axis=1)], axis=0
@@ -213,7 +227,7 @@
         acc = jnp.zeros((16, 2 * slots), jnp.float32)
         for k in range(0, width, 2):
             pair = sources[k : k + 2]
-            x = jnp.concatenate([feats[s] for s in pair], axis=1)
+            x = jnp.where(first_half, feats[pair[0], :, 0 : 2 * ROWS], feats[pair[-1], :, 0 : 2 * ROWS])
             z = jnp.concatenate([moms[s] for s in pair], axis=1)
             inv = lax.rsqrt(jnp.dot(x, both, preferred_element_type=jnp.float32))
             weight = inv * inv * inv
@@ -258,7 +272,7 @@
         live = lane4 < counts[iy, iz, ix]
         error = jnp.where(live & (row4 < 3), step + there - predicted, 0.0)
         for r in range(3):
-            drift_ref[pl.ds(3 * n + r, 1), :] = error[r : r + 1]
+            ends[pl.ds(3 * n + r, 1), :] = error[r : r + 1]
         summed = jnp.sum(error * error, axis=0, keepdims=True)
         squared[pl.ds(n, 1), :] = summed
         return stats + jnp.where(row8 == 0, summed, jnp.where((row8 == 1) & live[0:1], 1.0, 0.0))
@@ -272,6 +286,8 @@
 
     stats = lax.fori_loop(0, cells // group, several, jnp.zeros((8, slots), jnp.float32))
     stat[...] = stats[0:2]
+    keep = pltpu.make_async_copy(ends, ends_hbm, end_sem.at[0])
+    keep.start()
 
     def report(step, who):
         pltpu.make_async_remote_copy(
@@ -283,12 +299,16 @@
             device_id_type=MESH,
         ).start()
 
-    each_peer(report)
+    each_peer(report, outward=False)
     pltpu.make_async_copy(inbox, inbox, stat_recv).wait()
     sums = stat[...] + jnp.sum(inbox[...], axis=0)
     mean_sq = jnp.sum(sums[0:1], axis=1, keepdims=True) / jnp.sum(sums[1:2], axis=1, keepdims=True)
-    tension_ref[...] = squared[...] / (mean_sq + 1e-06)
+    tension[...] = squared[...] / (mean_sq + 1e-06)
+    last = pltpu.make_async_copy(tension, tension_hbm, end_sem.at[1])
+    last.start()
     pltpu.make_async_copy(inbox, inbox, stat_send).wait()
+    keep.wait()
+    last.wait()
 
 
 def shards(positions_now, velocities, positions_next, halo_counts, neighbour_lists, descendants):
@@ -305,15 +325,17 @@
     def rows(array):
         return jnp.transpose(array, (0, 1, 2, 3, 4)).reshape(cells * 3, slots)
 
-    drift, tension = pl.pallas_call(
+    ends, tension = pl.pallas_call(
         functools.partial(kernel, (cx, cy, cz), width, sizes),
         out_shape=(
             jax.ShapeDtypeStruct((cells * 3, slots), jnp.float32),
             jax.ShapeDtypeStruct((cells, slots), jnp.float32),
         ),
-        in_specs=[pl.BlockSpec(memory_space=pltpu.SMEM)] * 2 + [pl.BlockSpec(memory_space=pl.ANY)] * 4,
-        out_specs=(pl.BlockSpec(memory_space=pltpu.VMEM),) * 2,
+        in_specs=[pl.BlockSpec(memory_space=pl.ANY)] * 6,
+        out_specs=(pl.BlockSpec(memory_space=pl.ANY),) * 2,
         scratch_shapes=[
+            pltpu.SMEM((cells, 1, width), jnp.int32),
+            pltpu.SMEM((cy, cz, cx), jnp.int32),
             pltpu.VMEM((cells, 4, slots), jnp.float32),
             pltpu.VMEM((cells * 3, slots), jnp.float32),
             pltpu.VMEM((cells * 3, slots), jnp.float32),
@@ -323,10 +345,13 @@
             pltpu.VMEM((padded, slots, slots), jnp.bfloat16),
             pltpu.VMEM((padded, 16, slots), jnp.bfloat16),
             pltpu.VMEM((cells, ROWS, slots), jnp.bfloat16),
+            pltpu.VMEM((cells * 3, slots), jnp.float32),
+            pltpu.VMEM((cells, slots), jnp.float32),
             pltpu.VMEM((cells, slots), jnp.float32),
             pltpu.VMEM((2, slots), jnp.float32),
             pltpu.VMEM((peers, 2, slots), jnp.float32),
-            pltpu.SemaphoreType.DMA((4,)),
+            pltpu.SemaphoreType.DMA((6,)),
+            pltpu.SemaphoreType.DMA((2,)),
             pltpu.SemaphoreType.DMA((ways,)),
             pltpu.SemaphoreType.DMA((ways,)),
             pltpu.SemaphoreType.DMA((ways,)),
@@ -343,6 +368,7 @@
         rows(velocities),
         descendants.reshape(cells, 2, slots),
     )
+    drift = ends
     return (drift.reshape(cx, cy, cz, 3, slots), tension.reshape(cx, cy, cz, slots))
 
 

time: 34.1 us -> 30 us (0.88)
  Pallas kernels: 31.1 us -> 27.1 us
    pallas_call x1, Pallas kernels: 31.1 us -> 27.1 us  [shards(): pl.pallas_call(functools.partial(kernel, (cx, cy, cz), width, sizes), out...]
where the time goes in v3:
time: 30 us; the launch traced here: 29.8 us
  Pallas kernels  27.1 us (90%)
  local copies, waits for them, and re-layouts  2.06 us (7%)
  between operations  0.65 us (2%)
    pallas_call x1, Pallas kernels, shards(): pl.pallas_call(functools.partial(kernel, (cx, cy, cz), width, sizes), out...  27.1 us
    unnamed x4, local copies, waits for them, and re-layouts  2.06 us

profile of v3, /device:TPU:0, one launch (start us, length us, event | category | flops | bytes accessed | tf_op | source)
XLA Modules:
  0.0 29.8 jit_solution(13357976233620658874)
XLA Ops:
  0.6 27.1 %shard_map.77 = (f32[96,128]{1,0:T(8,128)}, f32[32,128]{1,0:T(8,128)}) custom-call(s32[32,1,14]{2,1,0:T(1,128)} %bitcast.16, s32[4,1,8]{2,1,0:T(1,128)} %bitcast.17, f32[32,4,128]{2,1,0:T(4,128)} %bitcast.10, f32[96,128]{1,0:T(8,128)} %bitcast.12, f32[96,128]{1,0:T(8,128)} %bitcast.13, s32[32,2,128]{2,1,0:T(2,128)} %bitcast.14), custom_call_target="tpu_custom_call" | custom-call | tf_op jit(solution)/shard_map/pallas_call | solution.py:328
  27.7 0.0 copy-start
  27.7 1.4 %copy.14 = f32[8,4,1,3,128]{4,2,3,1,0:T(1,128)} copy(f32[8,4,1,3,128]{4,2,3,1,0:T(1,128)} %bitcast.11) | data formatting | bytes 98304
  29.2 0.0 copy-done
  29.2 0.6 %copy.15 = f32[8,4,1,128]{3,2,1,0:T(1,128)} copy(f32[8,4,1,128]{3,2,1,0:T(1,128)S(1)} %bitcast.15) | data formatting | bytes 32768
Async XLA Ops:
  27.7 1.5 %copy-start = (f32[32,128]{1,0:T(8,128)S(1)}, f32[32,128]{1,0:T(8,128)}, u32[]{:S(2)}) copy-start(f32[32,128]{1,0:T(8,128)} %get-tuple-element.5) | copy-start | bytes 49156

commit v4 on v3

--- a/solution.py
+++ b/solution.py
@@ -234,7 +234,7 @@
             high = weight.astype(jnp.bfloat16)
             low = (weight - high.astype(jnp.float32)).astype(jnp.bfloat16)
             w = jnp.concatenate(
-                [jnp.concatenate([high[:, h * slots : (h + 1) * slots], low[:, h * slots : (h + 1) * slots]], axis=1) for h in range(2)], axis=0
+                [jnp.concatenate([high[:, h * slots : (h + 1) * slots], low[:, h * slots : (h + 1) * slots]], axis=1) for h in range(len(pair))], axis=0
             )
             acc += jnp.dot(z, w, preferred_element_type=jnp.float32)
         acc = acc[:, :slots] + acc[:, slots:]
@@ -309,6 +309,19 @@
     pltpu.make_async_copy(inbox, inbox, stat_send).wait()
     keep.wait()
     last.wait()
+
+
+def hand_over(drift_in, tension_in, drift_out, tension_out, drift_mid, tension_mid, sems):
+    ways = ((drift_in, drift_mid, drift_out), (tension_in, tension_mid, tension_out))
+    came = [pltpu.make_async_copy(src, mid, sems.at[i]) for i, (src, mid, _) in enumerate(ways)]
+    gone = [pltpu.make_async_copy(mid, dst, sems.at[2 + i]) for i, (_, mid, dst) in enumerate(ways)]
+    for copy in came:
+        copy.start()
+    for copy, onward in zip(came, gone):
+        copy.wait()
+        onward.start()
+    for onward in gone:
+        onward.wait()
 
 
 def shards(positions_now, velocities, positions_next, halo_counts, neighbour_lists, descendants):
@@ -368,7 +381,20 @@
         rows(velocities),
         descendants.reshape(cells, 2, slots),
     )
-    drift = ends
+    drift, tension = pl.pallas_call(
+        hand_over,
+        out_shape=(
+            jax.ShapeDtypeStruct((cells * 3, slots), jnp.float32),
+            jax.ShapeDtypeStruct((cells, slots), jnp.float32),
+        ),
+        in_specs=[pl.BlockSpec(memory_space=pl.ANY)] * 2,
+        out_specs=(pl.BlockSpec(memory_space=pl.ANY),) * 2,
+        scratch_shapes=[
+            pltpu.VMEM((cells * 3, slots), jnp.float32),
+            pltpu.VMEM((cells, slots), jnp.float32),
+            pltpu.SemaphoreType.DMA((4,)),
+        ],
+    )(ends, tension)
     return (drift.reshape(cx, cy, cz, 3, slots), tension.reshape(cx, cy, cz, slots))
 
 

time: 30 us -> 29.4 us (0.980)
  local copies, waits for them, and re-layouts: 2.06 us -> 0 us
  Pallas kernels: 27.1 us -> 28.5 us
    unnamed x4 -> x0, local copies, waits for them, and re-layouts: 2.06 us -> none
    pallas_call x0 -> x1, Pallas kernels: none -> 1.45 us  [shards(): pl.pallas_call(hand_over, out_shape=(jax.ShapeDtypeStruct((cells * 3, slo...]
where the time goes in v4:
time: 29.4 us; the launch traced here: 29.2 us
  Pallas kernels  28.5 us (97%)
  between operations  0.64 us (2%)
    pallas_call x1, Pallas kernels, shards(): pl.pallas_call(functools.partial(kernel, (cx, cy, cz), width, sizes), out...  27.1 us
    pallas_call x1, Pallas kernels, shards(): pl.pallas_call(hand_over, out_shape=(jax.ShapeDtypeStruct((cells * 3, slo...  1.45 us

profile of v4, /device:TPU:0, one launch (start us, length us, event | category | flops | bytes accessed | tf_op | source)
XLA Modules:
  0.0 29.2 jit_solution(13090070373120050451)
XLA Ops:
  0.6 27.1 %shard_map.77 = (f32[96,128]{1,0:T(8,128)}, f32[32,128]{1,0:T(8,128)}) custom-call(s32[32,1,14]{2,1,0:T(1,128)} %bitcast.14, s32[4,1,8]{2,1,0:T(1,128)} %bitcast.15, f32[32,4,128]{2,1,0:T(4,128)} %bitcast.10, f32[96,128]{1,0:T(8,128)} %bitcast.11, f32[96,128]{1,0:T(8,128)} %bitcast.12, s32[32,2,128]{2,1,0:T(2,128)} %bitcast.13), custom_call_target="tpu_custom_call" | custom-call | tf_op jit(solution)/shard_map/pallas_call | solution.py:341
  27.7 1.5 %shard_map.78 = (f32[96,128]{1,0:T(8,128)}, f32[32,128]{1,0:T(8,128)}) custom-call(f32[96,128]{1,0:T(8,128)} %get-tuple-element.6.drift_in, f32[32,128]{1,0:T(8,128)} %get-tuple-element.7.tension_in), custom_call_target="tpu_custom_call" | custom-call | tf_op jit(solution)/shard_map/pallas_call | solution.py:384
